TPU v7x, 32 devices: a whole 2x2x4 slice. The times are simulated.
32 devices in a mesh: row: 8 (over y, x, core), col: 4 (over z).
Axes of the slice: x: 2, y: 2, z: 4, core: 2. Of those that a mesh axis runs over, the one named last changes fastest.
Arguments:
- queries: bfloat16 [8, 128, 4096], P(None, 'row', 'col'), may hold values from -13 to 13, as said below
- key_cache: bfloat16 [8, 16384, 1024], P(None, ('row', 'col')), may hold values from -13 to 13
- value_cache: bfloat16 [8, 16384, 1024], P(None, ('row', 'col')), may hold values from -6 to 6
- key_table: bfloat16 [1024, 1024], replicated, may hold values from -24 to 24
- value_table: bfloat16 [1024, 1024], replicated, may hold values from -6 to 6
- lengths: int32 [8], replicated, may hold values from 2048 to 16384
- token_ids: int32 [8, 128], P(None, 'row'), may hold values from 0 to 1023
Outputs:
- attended: bfloat16 [8, 128, 4096], P(None, 'row', 'col')
Inputs may be any that keep to these rules, and one draw needn't show every extreme that they name: `queries`: entries of the query array lie in the stated range.
All inputs are finite; a program needn't handle non-finite values.
Results may differ from a plain program's by a relative error of at most 0.006.
Values may be sent and summed in bfloat16 or wider, within the bound.
A program may use at most 192 MiB of HBM per device.

v0:
```python
import functools
import math

import jax
import jax.numpy as jnp
from jax import lax
from jax.experimental import pallas as pl
from jax.experimental.pallas import tpu as pltpu
from jax.sharding import PartitionSpec as P

HQ = 32
KH = 8
HD = 128
GROUP = HQ // KH
CHUNKS = 2
LOG2E = math.log2(math.e)
MESH = pl.DeviceIdType.MESH


def attend_kernel(live_ref, q_ref, k_ref, v_ref, o_ref, m_ref, l_ref):
    rows, cols, _, piece, _ = q_ref.shape
    positions = k_ref.shape[1]
    kv_part = KH // cols
    part = piece // kv_part
    factor = HD ** (-0.5) * LOG2E
    live = live_ref[pl.program_id(0)]

    def run(masked):
        if masked:
            keep = lax.broadcasted_iota(jnp.int32, (positions, rows * part), 0) < live
        for j in range(KH):
            c, at = divmod(j, kv_part)
            span = slice(at * part, (at + 1) * part)
            q = q_ref[:, c, 0, span, :].reshape(rows * part, HD)
            k = k_ref[0, :, j * HD : (j + 1) * HD]
            s = lax.dot_general(k, q, (((1,), (1,)), ((), ())), preferred_element_type=jnp.float32)
            if masked:
                s = jnp.where(keep, s, -1e30)
            m = jnp.max(s, axis=0, keepdims=True)
            p = jnp.exp2((s - m) * factor)
            l_ref[0, j : j + 1, :] = jnp.sum(p, axis=0, keepdims=True)
            m_ref[0, j : j + 1, :] = m * factor
            v = v_ref[0, :, j * HD : (j + 1) * HD]
            o = lax.dot_general(
                v, p.astype(jnp.bfloat16), (((0,), (0,)), ((), ())), preferred_element_type=jnp.float32
            )
            o_ref[:, c, 0, span, :] = o.T.astype(jnp.bfloat16).reshape(rows, part, HD)

    @pl.when(live >= positions)
    def _():
        run(False)

    @pl.when((live > 0) & (live < positions))
    def _():
        run(True)

    @pl.when(live <= 0)
    def _():
        o_ref[...] = jnp.zeros_like(o_ref)
        m_ref[...] = jnp.full_like(m_ref, -1e30)
        l_ref[...] = jnp.zeros_like(l_ref)


def attend(live, gathered, keys, values, first):
    rows, cols, users, piece, _ = gathered.shape
    _, positions, width = keys.shape
    stat = rows * piece * cols // KH
    q_spec = pl.BlockSpec((rows, cols, 1, piece, HD), lambda u, live: (0, 0, u, 0, 0))
    c_spec = pl.BlockSpec((1, positions, width), lambda u, live: (u + first, 0, 0))
    s_spec = pl.BlockSpec((1, KH, stat), lambda u, live: (u, 0, 0))
    scores = users * KH * stat * positions
    return pl.pallas_call(
        attend_kernel,
        grid_spec=pltpu.PrefetchScalarGridSpec(
            num_scalar_prefetch=1,
            grid=(users,),
            in_specs=[q_spec, c_spec, c_spec],
            out_specs=[q_spec, s_spec, s_spec],
        ),
        out_shape=[
            jax.ShapeDtypeStruct(gathered.shape, jnp.bfloat16),
            jax.ShapeDtypeStruct((users, KH, stat), jnp.float32),
            jax.ShapeDtypeStruct((users, KH, stat), jnp.float32),
        ],
        compiler_params=pltpu.CompilerParams(
            dimension_semantics=("arbitrary",), vmem_limit_bytes=40 * 1024 * 1024
        ),
        cost_estimate=pl.CostEstimate(
            flops=4 * scores * HD * 2,
            bytes_accessed=4 * gathered.size + 4 * users * positions * width,
            transcendentals=scores,
        ),
        name="attend",
    )(live, gathered, keys, values)


def merge(pieces, n):
    peak = functools.reduce(jnp.maximum, [x[:n] for x in pieces])
    total = sum(x[n:] * jnp.exp2(x[:n] - peak) for x in pieces)
    return peak, total


def peaks_kernel(
    st_ref, all_ref, own_ref, row_in, col_out, col_in, row_all, send_sem, recv_sem
):
    rows, cols, two, _ = st_ref.shape
    n = two // 2
    me = {"row": lax.axis_index("row"), "col": lax.axis_index("col")}
    size = {"row": rows, "col": cols}

    def peer(axis, step):
        return {axis: lax.rem(me[axis] + step, size[axis])}

    others = [(axis, step) for axis in ("row", "col") for step in range(1, size[axis])]
    barrier = pltpu.get_barrier_semaphore()
    for axis, step in others:
        pl.semaphore_signal(barrier, inc=1, device_id=peer(axis, step), device_id_type=MESH)
    pl.semaphore_wait(barrier, len(others))

    taken = [0]

    def exchange(axis, source, target):
        copies = []
        for step in range(1, size[axis]):
            to = peer(axis, step)
            copy = pltpu.make_async_remote_copy(
                src_ref=source(to[axis]),
                dst_ref=target(step),
                send_sem=send_sem.at[taken[0]],
                recv_sem=recv_sem.at[taken[0]],
                device_id=to,
                device_id_type=MESH,
            )
            taken[0] += 1
            copy.start()
            copies.append(copy)
        for copy in copies:
            copy.wait()

    exchange("row", lambda to: st_ref.at[to], lambda step: row_in.at[step - 1])
    mine = st_ref[me["row"]]
    for c in range(cols):
        peak, total = merge([mine[c]] + [row_in[step, c] for step in range(rows - 1)], n)
        col_out[c, :n] = peak
        col_out[c, n:] = total
    exchange("col", lambda to: col_out.at[to], lambda step: col_in.at[step - 1])
    peak, total = merge([col_out[me["col"]]] + [col_in[step] for step in range(cols - 1)], n)
    own_ref[:n] = peak
    own_ref[n:] = total
    here = row_all.at[me["row"]]
    here[me["col"]] = peak
    spot = here.at[me["col"]]
    exchange("col", lambda to: spot, lambda step: spot)
    exchange("row", lambda to: here, lambda step: here)
    all_ref[...] = row_all[...]


def peaks(stats):
    rows, cols, two, lanes = stats.shape
    n = two // 2
    sends = 2 * (rows - 1) + 2 * (cols - 1)
    vmem = pl.BlockSpec(memory_space=pltpu.VMEM)
    return pl.pallas_call(
        peaks_kernel,
        out_shape=[
            jax.ShapeDtypeStruct((rows, cols, n, lanes), jnp.float32),
            jax.ShapeDtypeStruct((two, lanes), jnp.float32),
        ],
        in_specs=[vmem],
        out_specs=[vmem, vmem],
        scratch_shapes=[
            pltpu.VMEM((rows - 1, cols, two, lanes), jnp.float32),
            pltpu.VMEM((cols, two, lanes), jnp.float32),
            pltpu.VMEM((cols - 1, two, lanes), jnp.float32),
            pltpu.VMEM((rows, cols, n, lanes), jnp.float32),
            pltpu.SemaphoreType.DMA((sends,)),
            pltpu.SemaphoreType.DMA((sends,)),
        ],
        compiler_params=pltpu.CompilerParams(collective_id=0, has_side_effects=True),
        name="peaks",
    )(stats)


def body(queries, key_cache, value_cache, key_table, value_table, lengths, token_ids):
    users, beam_part, width_part = queries.shape
    heads_part = width_part // HD
    kv_part = heads_part // GROUP
    rows, cols = lax.axis_size("row"), lax.axis_size("col")
    row_at, col_at = lax.axis_index("row"), lax.axis_index("col")
    positions = key_cache.shape[1]
    offset = (row_at * cols + col_at) * positions
    live = jnp.clip(lengths - offset, 0, positions)
    piece = heads_part * beam_part
    q_local = queries.reshape(users, beam_part, heads_part, HD).transpose(0, 2, 1, 3)
    q_local = q_local.reshape(users, piece, HD)
    some = users // CHUNKS

    gathered = [
        lax.all_gather(lax.all_gather(q_local[i * some : (i + 1) * some], "col"), "row")
        for i in range(CHUNKS)
    ]

    own_keys, own_values = (
        jnp.einsum(
            "uwv,vc->uwc",
            (token_ids[..., None] == jnp.arange(table.shape[0], dtype=jnp.int32)).astype(jnp.bfloat16),
            lax.dynamic_slice_in_dim(table, col_at * kv_part * HD, kv_part * HD, 1),
            preferred_element_type=jnp.float32,
        )
        .reshape(users, beam_part, kv_part, HD)
        .transpose(0, 2, 1, 3)[:, :, None]
        for table in (key_table, value_table)
    )
    q_heads = q_local.astype(jnp.float32).reshape(users, kv_part, GROUP, beam_part, HD)
    own_score = jnp.sum(q_heads * own_keys, axis=-1) * (HD ** (-0.5) * LOG2E)

    sent, owns = [], []
    for i in range(CHUNKS):
        span = slice(i * some, (i + 1) * some)
        numer, m, l = attend(
            live[span],
            gathered[i],
            key_cache,
            value_cache,
            i * some,
        )

        def by_device(x):
            x = x.reshape(some, cols, kv_part, rows, piece // kv_part)
            return x.transpose(3, 1, 0, 2, 4).reshape(rows, cols, some * piece // HD, HD)

        m = by_device(m)
        peak_all, own = peaks(jnp.concatenate([m, by_device(l)], axis=2))
        factor = jnp.exp2(m - peak_all).reshape(rows, cols, some, piece)
        weighted = numer.astype(jnp.float32) * factor[..., None]
        sent.append(
            lax.psum_scatter(weighted.astype(jnp.bfloat16), "row", scatter_dimension=0, tiled=False)
        )
        owns.append(own.reshape(2, some, kv_part, GROUP, beam_part))

    numer = lax.psum_scatter(jnp.concatenate(sent, axis=1), "col", scatter_dimension=0, tiled=False)
    numer = numer.astype(jnp.float32).reshape(users, kv_part, GROUP, beam_part, HD)
    peak, total = jnp.concatenate(owns, axis=1)
    top = jnp.maximum(peak, own_score)
    carried = jnp.exp2(peak - top)
    fresh = jnp.exp2(own_score - top)
    numer = numer * carried[..., None] + fresh[..., None] * own_values
    result = numer / (total * carried + fresh)[..., None]
    result = result.reshape(users, heads_part, beam_part, HD)
    return result.transpose(0, 2, 1, 3).reshape(users, beam_part, width_part).astype(jnp.bfloat16)


def solution(mesh):
    return jax.shard_map(
        body,
        mesh=mesh,
        in_specs=(
            P(None, "row", "col"),
            P(None, ("row", "col"), None),
            P(None, ("row", "col"), None),
            P(),
            P(),
            P(),
            P(None, "row"),
        ),
        out_specs=P(None, "row", "col"),
        check_vma=False,
    )
```

profile of v0, /device:TPU:0, one launch (start us, length us, event | category | flops | bytes accessed | tf_op | source)
XLA Modules:
  0.0 261.2 jit_solution(1729439665493400822)
XLA Ops:
  6.5 1.2 copy.60
  7.8 18.0 %all_gather.29 = bf16[4,4,128,128]{3,2,1,0:T(8,128)(2,1)} all-gather(bf16[1,4,128,128]{3,2,1,0:T(8,128)(2,1)S(1)} %bitcast.58), channel_id=1, replica_groups=mesh['row'=8,'col'=4] {'col'}, dimensions={0}, use_global_device_ids=true | all-gather | bytes 655360 | tf_op jit(solution)/shard_map/all_gather | solution.py:199
  25.9 17.1 %all_gather.25 = bf16[4,4,128,128]{3,2,1,0:T(8,128)(2,1)} all-gather(bf16[1,4,128,128]{3,2,1,0:T(8,128)(2,1)S(1)} %bitcast.59), channel_id=1, replica_groups=mesh['row'=8,'col'=4] {'col'}, dimensions={0}, use_global_device_ids=true | all-gather | bytes 655360 | tf_op jit(solution)/shard_map/all_gather | solution.py:199
  43.2 21.3 %all-gather.7.cloned.1.call-done = bf16[32,4,128,128]{3,2,1,0:T(8,128)(2,1)} async-done(((bf16[4,4,128,128]{3,2,1,0:T(8,128)(2,1)}), bf16[32,4,128,128]{3,2,1,0:T(8,128)(2,1)}) %all-gather.7.cloned.1.call-update) | async-done | bytes 4194320 | tf_op jit(solution)/shard_map/all_gather | solution.py:199
  64.5 2.2 copy-done.4
  66.7 21.0 %attend.3 = (bf16[8,4,4,128,128]{4,3,2,1,0:T(8,128)(2,1)S(1)}, f32[4,8,512]{2,1,0:T(8,128)S(1)}, f32[4,8,512]{2,1,0:T(8,128)S(1)}) custom-call(s32[4]{0:T(128)S(1)} %get-tuple-element.33.live_ref, bf16[8,4,4,128,128]{4,3,2,1,0:T(8,128)(2,1)S(1)} %bitcast.52, bf16[8,512,1024]{2,1,0:T(8,128)(2,1)} %k_ref.3, bf16[8,512,1024]{2,1,0:T(8,128)(2,1)} %v_ref.3), custom_call_target="tpu_custom_call" | custom-call | flops 8589934592 | bytes 16777216 | tf_op jit(solution)/shard_map/attend/pallas_call | solution.py:72
  87.7 2.0 copy-done.1
  90.3 0.7 pad_maximum_fusion.2.st_ref
  91.0 20.2 %peaks.3 = (f32[8,4,4,128]{3,2,1,0:T(4,128)}, f32[8,128]{1,0:T(8,128)}) custom-call(f32[8,4,8,128]{3,2,1,0:T(8,128)} %pad_maximum_fusion.2.st_ref), custom_call_target="tpu_custom_call" | custom-call | tf_op jit(solution)/shard_map/peaks/pallas_call | solution.py:163
  111.2 0.9 multiply_exponential_fusion
  112.1 5.8 %multiply_convert_fusion = bf16[8,4,4,128,128]{4,3,2,1,0:T(8,128)(2,1)} fusion(bf16[8,4,4,128,128]{4,3,2,1,0:T(8,128)(2,1)} %copy-done.1, f32[8,4,4,128]{3,2,1,0:T(4,128)S(1)} %multiply_exponential_fusion), kind=kLoop, calls=%fused_computation | loop fusion | flops 6291456 | bytes 8454144 | tf_op jit(solution)/shard_map/convert_element_type | solution.py:237
  118.2 2.2 copy-done.3
  120.4 21.0 %attend.2 = (bf16[8,4,4,128,128]{4,3,2,1,0:T(8,128)(2,1)S(1)}, f32[4,8,512]{2,1,0:T(8,128)S(1)}, f32[4,8,512]{2,1,0:T(8,128)S(1)}) custom-call(s32[4]{0:T(128)S(1)} %get-tuple-element.32.live_ref, bf16[8,4,4,128,128]{4,3,2,1,0:T(8,128)(2,1)S(1)} %bitcast.51, bf16[8,512,1024]{2,1,0:T(8,128)(2,1)} %k_ref.3, bf16[8,512,1024]{2,1,0:T(8,128)(2,1)} %v_ref.3), custom_call_target="tpu_custom_call" | custom-call | flops 8589934592 | bytes 16777216 | tf_op jit(solution)/shard_map/attend/pallas_call | solution.py:72
  141.4 2.0 copy-done.2
  144.0 0.7 pad_maximum_fusion.1.st_ref
  144.7 18.5 %peaks.2 = (f32[8,4,4,128]{3,2,1,0:T(4,128)}, f32[8,128]{1,0:T(8,128)}) custom-call(f32[8,4,8,128]{3,2,1,0:T(8,128)} %pad_maximum_fusion.1.st_ref), custom_call_target="tpu_custom_call" | custom-call | tf_op jit(solution)/shard_map/peaks/pallas_call | solution.py:163
  163.2 0.9 multiply_exponential_fusion.1
  164.0 5.9 %multiply_convert_fusion.1 = bf16[8,4,4,128,128]{4,3,2,1,0:T(8,128)(2,1)} fusion(bf16[8,4,4,128,128]{4,3,2,1,0:T(8,128)(2,1)} %copy-done.2, f32[8,4,4,128]{3,2,1,0:T(4,128)S(1)} %multiply_exponential_fusion.1), kind=kLoop, calls=%fused_computation.1 | loop fusion | flops 6291456 | bytes 8454144 | tf_op jit(solution)/shard_map/convert_element_type | solution.py:237
  170.0 52.7 %reduce-scatter.4.cloned.1.call-done = bf16[1,4,4,128,128]{4,3,2,1,0:T(8,128)(2,1)} async-done(((bf16[8,4,4,128,128]{4,3,2,1,0:T(8,128)(2,1)}), bf16[1,4,4,128,128]{4,3,2,1,0:T(8,128)(2,1)}) %reduce-scatter.4.cloned.1.call-update) | async-done | bytes 524304 | tf_op jit(solution)/shard_map/reduce_scatter | solution.py:237
  222.8 2.3 pad_maximum_fusion
  225.1 0.3 fusion.5
  225.5 1.3 fusion.3
  227.6 24.9 %reduce-scatter.8.cloned.1.call-done = bf16[1,8,128,128]{3,2,1,0:T(8,128)(2,1)} async-done(((bf16[4,8,128,128]{3,2,1,0:T(8,128)(2,1)}), bf16[1,8,128,128]{3,2,1,0:T(8,128)(2,1)}) %reduce-scatter.8.cloned.1.call-update) | async-done | bytes 262160 | tf_op jit(solution)/shard_map/reduce_scatter | solution.py:241
  252.6 2.1 copy_bitcast_fusion
  (57 shorter events, 2.7 us)
Async XLA Ops:
  6.5 218.6 %copy-start = (bf16[1024,1024]{1,0:T(8,128)(2,1)S(1)}, bf16[1024,1024]{1,0:T(8,128)(2,1)}, u32[]{:S(2)}) copy-start(bf16[1024,1024]{1,0:T(8,128)(2,1)} %param.10) | copy-start | bytes 6291460
  6.5 36.5 %copy-start.8 = (s32[8]{0:T(128)S(1)}, s32[8]{0:T(128)}, u32[]{:S(2)}) copy-start(s32[8]{0:T(128)} %param.12) | copy-start | bytes 100
  6.5 58.0 %all-gather.7.cloned.1.call-start = ((), (), s32[]{:S(2)}) async-start(), calls=%async_computation.7 | async-start | bytes 4718592 | tf_op jit(solution)/shard_map/all_gather | solution.py:199
  25.8 92.4 %all-gather.5.cloned.1.call-start = ((), (), s32[]{:S(2)}) async-start(), calls=%async_computation.6 | async-start | bytes 4718592 | tf_op jit(solution)/shard_map/all_gather | solution.py:199
  43.0 127.0 %reduce-scatter.6.cloned.1.call-start = ((), (), s32[]{:S(2)}) async-start(), calls=%async_computation.4 | async-start | bytes 4718592 | tf_op jit(solution)/shard_map/reduce_scatter | solution.py:237
  64.5 2.2 copy-start.4
  87.7 2.0 copy-start.1
  117.9 104.9 %reduce-scatter.4.cloned.1.call-start = ((), (), s32[]{:S(2)}) async-start(), calls=%async_computation.3 | async-start | bytes 4718592 | tf_op jit(solution)/shard_map/reduce_scatter | solution.py:237
  118.2 2.2 copy-start.3
  141.4 2.0 copy-start.2
  169.9 55.2 %copy-start.5 = (s32[8,16]{1,0:T(8,128)S(1)}, s32[8,16]{1,0:T(8,128)}, u32[]{:S(2)}) copy-start(s32[8,16]{1,0:T(8,128)} %param.13) | copy-start | bytes 1540
  170.0 57.4 %copy-start.6 = (f32[8,128]{1,0:T(8,128)S(1)}, f32[8,128]{1,0:T(8,128)}, u32[]{:S(2)}) copy-start(f32[8,128]{1,0:T(8,128)} %get-tuple-element.24) | copy-start | bytes 12292
  170.0 57.5 %copy-start.7 = (f32[8,128]{1,0:T(8,128)S(1)}, f32[8,128]{1,0:T(8,128)}, u32[]{:S(2)}) copy-start(f32[8,128]{1,0:T(8,128)} %get-tuple-element.23) | copy-start | bytes 12292
  170.0 82.6 %reduce-scatter.8.cloned.1.call-start = ((), (), s32[]{:S(2)}) async-start(), calls=%async_computation.5 | async-start | bytes 1310720 | tf_op jit(solution)/shard_map/reduce_scatter | solution.py:241
Sparse Core Ops, SparseCore 0:
  25.9 38.5 all-gather.6
  66.4 37.9 all-gather.4
  118.0 50.6 reduce-scatter.5
  171.9 50.8 reduce-scatter.3
  225.2 27.2 reduce-scatter.7
where the time goes:
time: 262 us; the launch traced here: 261 us
  waiting for transfers between devices  99.1 us (38%)
  Pallas kernels  80.7 us (31%)
  blocking collectives  35.1 us (13%)
  other arithmetic  19.5 us (7%)
  between operations  13.5 us (5%)
  local copies, waits for them, and re-layouts  11.4 us (4%)
    reduce_scatter x2, waiting for transfers between devices, body(): lax.psum_scatter(weighted.astype(jnp.bfloat16), 'row', scatter_dimension=...  52.8 us
    pallas_call x2, Pallas kernels, attend(): pl.pallas_call(attend_kernel, grid_spec=pltpu.PrefetchScalarGridSpec(num_...  42 us
    pallas_call x2, Pallas kernels, peaks(): pl.pallas_call(peaks_kernel, out_shape=[jax.ShapeDtypeStruct((rows, cols,...  38.7 us
    all_gather x2, blocking collectives, body(): lax.all_gather(q_local[i * some:(i + 1) * some], 'col')  35.1 us
    reduce_scatter x1, waiting for transfers between devices, body(): lax.psum_scatter(jnp.concatenate(sent, axis=1), 'col', scatter_dimension=...  24.9 us
    all_gather x2, waiting for transfers between devices, body(): lax.all_gather(lax.all_gather(q_local[i * some:(i + 1) * some], 'col'), '...  21.4 us
    convert_element_type x2, other arithmetic, body(): weighted.astype(jnp.bfloat16)  11.7 us
    unnamed x19, local copies, waits for them, and re-layouts  9.48 us
  transfers between devices with their start and end apart: 5, of which 3 were waited for; matrix products, arithmetic and copies ran while one was open for 7% of the time, Pallas kernels for 31%

commit v1 on v0

v1 whole, which is shorter than its diff:
```python
import math

import jax
import jax.numpy as jnp
from jax import lax
from jax.experimental import pallas as pl
from jax.experimental.pallas import tpu as pltpu
from jax.sharding import PartitionSpec as P

HQ = 32
KH = 8
HD = 128
GROUP = HQ // KH
CORES = 2
LOG2E = math.log2(math.e)
FACTOR = HD ** (-0.5) * LOG2E
MESH = pl.DeviceIdType.MESH
LEAD = 3
TAIL = 3


class Plan:
    def __init__(self, rows, cols):
        self.rows, self.cols = rows, cols
        self.planes = rows // CORES
        self.outer = 2 if self.planes % 2 == 0 else 1
        self.inner = self.planes // self.outer
        self.half = cols // 2
        names = []
        for s in range(1, cols):
            names += [("z", s), ("zr", s), ("zs", s)]
        for b in range(1, self.inner):
            names += [("bx", b), ("cd", b), ("x", b), ("xs", b)]
        for a in range(1, self.outer):
            names += [("by", a), ("ce", a), ("y", a), ("ys", a)]
            for b in range(1, self.inner):
                names += [(n, a, b) for n in ("ca", "cb", "dd", "ra", "ras", "rb", "rbs")]
        names += [("bd",), ("f",), ("fs",), ("fo",)]
        self.index = {name: at for at, name in enumerate(names)}


def step_kernel(
    plan, live_ref, q_in, k_hbm, v_hbm, out_ref, st_out,
    q_all, part, from_pair, st, st_pair, sc, ra, ras, rb, rbs, xr, xrs, yr, yrs, zr, zrs, fin,
    kbuf, vbuf, send, recv, local,
):
    users = q_in.shape[0]
    outer, inner, cols, half = plan.outer, plan.inner, plan.cols, plan.half
    planes = plan.planes
    kv = KH // cols
    lines = q_in.shape[1] // kv
    lanes = CORES * lines
    positions = k_hbm.shape[1]
    row, col = lax.axis_index("row"), lax.axis_index("col")
    k = lax.rem(row, CORES)
    pair = 1 - k
    me = row // CORES
    b_at, a_at = lax.rem(me, inner), me // inner

    def spot(a=0, b=0):
        return lax.rem(a_at + a + outer, outer) * inner + lax.rem(b_at + b + inner, inner)

    def at_spot(a=0, b=0):
        return {"row": spot(a, b) * CORES + k}

    def at_col(s):
        return {"col": lax.rem(col + s, cols)}

    at_pair = {"row": me * CORES + pair}
    in_x = range(1, inner)
    in_y = range(1, outer)
    in_xy = [(a, b) for a in in_y for b in in_x]
    in_z = range(1, cols)

    peers = [at_pair] + [at_col(s) for s in in_z] + [at_spot(0, b) for b in in_x] + [at_spot(a, 0) for a in in_y]

    def copy(v, name, src, dst, to):
        at = plan.index[name]
        return pltpu.make_async_remote_copy(
            src_ref=src, dst_ref=dst, send_sem=send.at[v, at], recv_sem=recv.at[v, at],
            device_id=to, device_id_type=MESH,
        )

    low, high = pl.ds(0, half), pl.ds(half, cols - half)

    def make(v, name):
        kind, *at = name
        if kind == "z":
            return copy(v, name, q_in.at[v], q_all.at[v, me, k, col], at_col(at[0]))
        if kind in ("bx", "by", "bd"):
            to = at_pair if kind == "bd" else at_spot(0, at[0]) if kind == "bx" else at_spot(at[0], 0)
            own = q_all.at[v, me, k]
            return copy(v, name, own, own, to)
        if kind == "cd":
            ref = q_all.at[v, spot(0, -at[0]), k]
            return copy(v, name, ref, ref, at_pair)
        if kind == "ce":
            ref = q_all.at[v, spot(-at[0], 0), k]
            return copy(v, name, ref, ref, at_pair)
        if kind == "ca":
            ref = q_all.at[v, spot(0, -at[1]), k, low]
            return copy(v, name, ref, ref, at_spot(at[0], 0))
        if kind == "cb":
            ref = q_all.at[v, spot(-at[0], 0), k, high]
            return copy(v, name, ref, ref, at_spot(0, at[1]))
        if kind == "dd":
            ref = q_all.at[v, spot(-at[0], -at[1]), k]
            return copy(v, name, ref, ref, at_pair)
        if kind == "f":
            return copy(v, name, part.at[v, pair], from_pair.at[v], at_pair)
        if kind == "fs":
            return copy(v, name, st.at[v], st_pair.at[v], at_pair)
        if kind == "ra":
            return copy(v, name, part.at[v, k, spot(*at), low], ra.at[v, at[0] - 1, at[1] - 1], at_spot(at[0], 0))
        if kind == "ras":
            return copy(v, name, sc.at[v, spot(*at), low], ras.at[v, at[0] - 1, at[1] - 1], at_spot(at[0], 0))
        if kind == "rb":
            return copy(v, name, part.at[v, k, spot(*at), high], rb.at[v, at[0] - 1, at[1] - 1], at_spot(0, at[1]))
        if kind == "rbs":
            return copy(v, name, sc.at[v, spot(*at), high], rbs.at[v, at[0] - 1, at[1] - 1], at_spot(0, at[1]))
        if kind == "x":
            return copy(v, name, part.at[v, k, spot(0, at[0])], xr.at[v, at[0] - 1], at_spot(0, at[0]))
        if kind == "xs":
            return copy(v, name, sc.at[v, spot(0, at[0])], xrs.at[v, at[0] - 1], at_spot(0, at[0]))
        if kind == "y":
            return copy(v, name, part.at[v, k, spot(at[0], 0)], yr.at[v, at[0] - 1], at_spot(at[0], 0))
        if kind == "ys":
            return copy(v, name, sc.at[v, spot(at[0], 0)], yrs.at[v, at[0] - 1], at_spot(at[0], 0))
        if kind == "zr":
            there = lax.rem(col + at[0], cols)
            return copy(v, name, part.at[v, k, me, there], zr.at[v, at[0] - 1], at_col(at[0]))
        if kind == "zs":
            there = lax.rem(col + at[0], cols)
            return copy(v, name, sc.at[v, me, there], zrs.at[v, at[0] - 1], at_col(at[0]))
        return copy(v, name, fin.at[v, k], fin.at[v, k], at_pair)

    def start(v, *names):
        for name in names:
            make(v, name).start()

    def arrived(v, *names):
        for name in names:
            make(v, name).wait_recv()

    def when(v, fn):
        @pl.when((v >= 0) & (v < users))
        def _():
            fn(v)

    def own_copy():
        return pltpu.make_async_copy(q_in, q_all.at[:, me, k, col], local.at[0])

    def fetch(v):
        slot = lax.rem(v, 2)
        return (
            pltpu.make_async_copy(k_hbm.at[v], kbuf.at[slot], local.at[1 + slot]),
            pltpu.make_async_copy(v_hbm.at[v], vbuf.at[slot], local.at[3 + slot]),
        )

    def start_fetch(v):
        for c in fetch(v):
            c.start()

    def columns(v):
        arrived(v, *[("z", s) for s in in_z])
        start(v, *[("bx", b) for b in in_x], *[("by", a) for a in in_y], ("bd",))

    def relay(v):
        for b in in_x:
            arrived(v, ("bx", b))
            start(v, *[("ca", a, b) for a in in_y], ("cd", b))
        for a in in_y:
            arrived(v, ("by", a))
            start(v, *[("cb", a, b) for b in in_x], ("ce", a))

    def diagonal(v):
        for a, b in in_xy:
            arrived(v, ("ca", a, b), ("cb", a, b))
            start(v, ("dd", a, b))

    def gathered(v):
        arrived(v, ("bd",), *[("cd", b) for b in in_x], *[("ce", a) for a in in_y])
        arrived(v, *[("dd", a, b) for a, b in in_xy])

    def heads(v, some):
        slot = lax.rem(v, 2)
        keep = lax.broadcasted_iota(jnp.int32, (positions, planes * lanes), 0) < live_ref[v]
        for j in some:
            c, i = divmod(j, kv)
            q = q_all[v, :, :, c, i * lines : (i + 1) * lines, :].reshape(planes * lanes, HD)
            keys = kbuf[slot, :, j * HD : (j + 1) * HD]
            s = lax.dot_general(keys, q, (((1,), (1,)), ((), ())), preferred_element_type=jnp.float32)
            s = jnp.where(keep, s, -1e30)
            m = jnp.max(s, axis=0, keepdims=True)
            p = jnp.exp2((s - m) * FACTOR)
            total = jnp.sum(p, axis=0, keepdims=True)
            m = m * FACTOR
            values = vbuf[slot, :, j * HD : (j + 1) * HD]
            o = lax.dot_general(
                values, p.astype(jnp.bfloat16), (((0,), (0,)), ((), ())), preferred_element_type=jnp.float32
            ).astype(jnp.bfloat16)
            for at in range(planes):
                span = slice(at * lanes, (at + 1) * lanes)
                st[v, at, c, i : i + 1, :] = m[:, span]
                st[v, at, c, kv + i : kv + i + 1, :] = total[:, span]
                for h in range(2):
                    part[v, h, at, c, i] = o[h * (HD // 2) : (h + 1) * (HD // 2), span]

    def fuse(numers, stats):
        peaks = [x[:kv] for x in stats]
        peak = peaks[0]
        for x in peaks[1:]:
            peak = jnp.maximum(peak, x)
        scales = [jnp.exp2(x - peak) for x in peaks]
        total = sum(x[kv:] * scale for x, scale in zip(stats, scales))
        sums = [
            sum(x[i].astype(jnp.float32) * scale[i : i + 1] for x, scale in zip(numers, scales))
            for i in range(kv)
        ]
        return sums, peak, total

    def fuse_into(v, at, c, numers, stats, first=None):
        own = part.at[v, k, at, c]
        own_st = sc.at[v, at, c]
        given = own_st if first is None else first
        sums, peak, total = fuse([own] + numers, [given[...]] + stats)
        for i in range(kv):
            own[i] = sums[i].astype(jnp.bfloat16)
        own_st[:kv] = peak
        own_st[kv:] = total

    def paired(v):
        arrived(v, ("f",), ("fs",))

        def one(at, _):
            for c in range(cols):
                fuse_into(v, at, c, [from_pair.at[v, at, c]], [st_pair[v, at, c]], st.at[v, at, c])
            return 0

        lax.fori_loop(0, planes, one, 0)
        for a, b in in_xy:
            start(v, ("ra", a, b), ("ras", a, b), ("rb", a, b), ("rbs", a, b))

    def crossed(v):
        for a, b in in_xy:
            arrived(v, ("ra", a, b), ("ras", a, b))
        for b in in_x:
            if in_y:
                for c in range(half):
                    fuse_into(
                        v, spot(0, b), c,
                        [ra.at[v, a - 1, b - 1, c] for a in in_y], [ras[v, a - 1, b - 1, c] for a in in_y],
                    )
            start(v, ("x", b), ("xs", b))
        for a, b in in_xy:
            arrived(v, ("rb", a, b), ("rbs", a, b))
        for a in in_y:
            if in_x:
                for c in range(cols - half):
                    fuse_into(
                        v, spot(a, 0), half + c,
                        [rb.at[v, a - 1, b - 1, c] for b in in_x], [rbs[v, a - 1, b - 1, c] for b in in_x],
                    )
            start(v, ("y", a), ("ys", a))

    def reduced(v):
        for b in in_x:
            arrived(v, ("x", b), ("xs", b))
        for a in in_y:
            arrived(v, ("y", a), ("ys", a))
        for c in range(cols):
            fuse_into(
                v, me, c,
                [xr.at[v, b - 1, c] for b in in_x] + [yr.at[v, a - 1, c] for a in in_y],
                [xrs[v, b - 1, c] for b in in_x] + [yrs[v, a - 1, c] for a in in_y],
            )
        for s in in_z:
            start(v, ("zr", s), ("zs", s))

    def finished(v):
        for s in in_z:
            arrived(v, ("zr", s), ("zs", s))
        sums, peak, total = fuse(
            [part.at[v, k, me, col]] + [zr.at[v, s - 1] for s in in_z],
            [sc[v, me, col]] + [zrs[v, s - 1] for s in in_z],
        )
        for i in range(kv):
            fin[v, k, i] = sums[i]
        st_out[v, :kv] = peak
        st_out[v, kv:] = total
        start(v, ("fo",))

    own_copy().start()
    start_fetch(0)
    barrier = pltpu.get_barrier_semaphore()
    for to in peers:
        pl.semaphore_signal(barrier, inc=1, device_id=to, device_id_type=MESH)
    pl.semaphore_wait(barrier, len(peers))

    def send_queries(v, _):
        start(v, *[("z", s) for s in in_z])
        return 0

    lax.fori_loop(0, users, send_queries, 0)
    own_copy().wait()

    def turn(t, _):
        u = t - LEAD
        when(u + 3, columns)

        @pl.when((u >= 0) & (u + 1 < users))
        def _():
            start_fetch(u + 1)

        def begin(v):
            gathered(v)
            for c in fetch(v):
                c.wait()
            heads(v, range(0, KH // 4))

        when(u, begin)
        when(u - 1, paired)
        when(u, lambda v: heads(v, range(KH // 4, KH // 2)))
        when(u + 2, relay)
        when(u - 2, reduced)
        when(u, lambda v: heads(v, range(KH // 2, 3 * KH // 4)))
        when(u - 1, crossed)

        def end(v):
            heads(v, range(3 * KH // 4, KH))
            start(v, ("f",), ("fs",))

        when(u, end)
        when(u + 1, diagonal)
        when(u - 3, finished)
        return 0

    lax.fori_loop(0, users + LEAD + TAIL, turn, 0)

    def close(v, _):
        arrived(v, ("fo",))
        out_ref[v] = fin[v]
        for name in plan.index:
            make(v, name).wait_send()
        return 0

    lax.fori_loop(0, users, close, 0)


def step(live, q_local, keys, values, rows, cols):
    users, piece, _ = q_local.shape
    plan = Plan(rows, cols)
    _, positions, width = keys.shape
    kv = KH // cols
    lanes = CORES * piece // kv
    outer, inner, planes, half = plan.outer, plan.inner, plan.planes, plan.half
    deep = HD // 2
    f32, bf16 = jnp.float32, jnp.bfloat16
    vmem = pl.BlockSpec(memory_space=pltpu.VMEM)
    hbm = pl.BlockSpec(memory_space=pl.ANY)
    block, stat = (kv, deep, lanes), (2 * kv, lanes)

    def numer(*lead):
        return pltpu.VMEM((users, *lead, *block), bf16)

    def stats(*lead):
        return pltpu.VMEM((users, *lead, *stat), f32)

    x, y = max(inner - 1, 1), max(outer - 1, 1)
    copies = len(plan.index)
    scores = users * KH * planes * lanes * positions
    return pl.pallas_call(
        lambda *refs: step_kernel(plan, *refs),
        out_shape=[
            jax.ShapeDtypeStruct((users, 2, *block), f32),
            jax.ShapeDtypeStruct((users, *stat), f32),
        ],
        in_specs=[pl.BlockSpec(memory_space=pltpu.SMEM), vmem, hbm, hbm],
        out_specs=[vmem, vmem],
        scratch_shapes=[
            pltpu.VMEM((users, planes, CORES, cols, piece, HD), bf16),
            numer(2, planes, cols),
            numer(planes, cols),
            stats(planes, cols),
            stats(planes, cols),
            stats(planes, cols),
            numer(y, x, half),
            stats(y, x, half),
            numer(y, x, cols - half),
            stats(y, x, cols - half),
            numer(x, cols),
            stats(x, cols),
            numer(y, cols),
            stats(y, cols),
            numer(cols - 1),
            stats(cols - 1),
            pltpu.VMEM((users, 2, *block), f32),
            pltpu.VMEM((2, positions, width), bf16),
            pltpu.VMEM((2, positions, width), bf16),
            pltpu.SemaphoreType.DMA((users, copies)),
            pltpu.SemaphoreType.DMA((users, copies)),
            pltpu.SemaphoreType.DMA((5,)),
        ],
        compiler_params=pltpu.CompilerParams(
            collective_id=0, has_side_effects=True, vmem_limit_bytes=60 * 1024 * 1024
        ),
        cost_estimate=pl.CostEstimate(
            flops=4 * scores * HD, bytes_accessed=4 * users * positions * width, transcendentals=scores
        ),
        name="step",
    )(live, q_local, keys, values)


def body(queries, key_cache, value_cache, key_table, value_table, lengths, token_ids):
    users, beam_part, width_part = queries.shape
    heads_part = width_part // HD
    kv_part = heads_part // GROUP
    rows, cols = lax.axis_size("row"), lax.axis_size("col")
    row_at, col_at = lax.axis_index("row"), lax.axis_index("col")
    positions = key_cache.shape[1]
    offset = (row_at * cols + col_at) * positions
    live = jnp.clip(lengths - offset, 0, positions)
    piece = heads_part * beam_part
    q_local = queries.reshape(users, beam_part, heads_part, HD).transpose(0, 2, 1, 3)
    q_local = q_local.reshape(users, piece, HD)

    own_keys, own_values = (
        jnp.einsum(
            "uwv,vc->uwc",
            (token_ids[..., None] == jnp.arange(table.shape[0], dtype=jnp.int32)).astype(jnp.bfloat16),
            lax.dynamic_slice_in_dim(table, col_at * kv_part * HD, kv_part * HD, 1),
            preferred_element_type=jnp.float32,
        )
        .reshape(users, beam_part, kv_part, HD)
        .transpose(0, 2, 1, 3)[:, :, None]
        for table in (key_table, value_table)
    )
    q_heads = q_local.astype(jnp.float32).reshape(users, kv_part, GROUP, beam_part, HD)
    own_score = jnp.sum(q_heads * own_keys, axis=-1) * FACTOR

    numer, stat = step(live, q_local, key_cache, value_cache, rows, cols)
    lines = GROUP * beam_part
    mine = lax.rem(row_at, CORES) * lines
    numer = lax.dynamic_slice_in_dim(numer, mine, lines, 4)
    numer = numer.transpose(0, 2, 4, 1, 3).reshape(users, kv_part, GROUP, beam_part, HD)
    stat = lax.dynamic_slice_in_dim(stat, mine, lines, 2).reshape(users, 2, kv_part, GROUP, beam_part)
    peak, total = stat[:, 0], stat[:, 1]
    top = jnp.maximum(peak, own_score)
    carried = jnp.exp2(peak - top)
    fresh = jnp.exp2(own_score - top)
    numer = numer * carried[..., None] + fresh[..., None] * own_values
    result = numer / (total * carried + fresh)[..., None]
    result = result.reshape(users, heads_part, beam_part, HD)
    return result.transpose(0, 2, 1, 3).reshape(users, beam_part, width_part).astype(jnp.bfloat16)


def solution(mesh):
    return jax.shard_map(
        body,
        mesh=mesh,
        in_specs=(
            P(None, "row", "col"),
            P(None, ("row", "col"), None),
            P(None, ("row", "col"), None),
            P(),
            P(),
            P(),
            P(None, "row"),
        ),
        out_specs=P(None, "row", "col"),
        check_vma=False,
    )
```

time: 262 us -> 123 us (0.47)
  waiting for transfers between devices: 99.1 us -> 0 us
  blocking collectives: 35.1 us -> 0 us
  Pallas kernels: 80.7 us -> 111 us
  other arithmetic: 19.5 us -> 2.82 us
  between operations: 13.5 us -> 0.18 us
  local copies, waits for them, and re-layouts: 11.4 us -> 6.87 us
    reduce_scatter x3 -> x0, waiting for transfers between devices: 77.7 us -> none  [the longest x2 52.8 us: body(): lax.psum_scatter(weighted.astype(jnp.bfloat16), 'row', scatter_dimension=...]
    all_gather x2 -> x0, blocking collectives: 35.1 us -> none  [body(): lax.all_gather(q_local[i * some:(i + 1) * some], 'col')]
    pallas_call x4 -> x1, Pallas kernels: 80.7 us -> 111 us  [step(): pl.pallas_call(lambda *refs: step_kernel(plan, *refs), out_shape=[jax.Sha...]
    all_gather x2 -> x0, waiting for transfers between devices: 21.4 us -> none  [body(): lax.all_gather(lax.all_gather(q_local[i * some:(i + 1) * some], 'col'), '...]
    convert_element_type x2 -> x0, other arithmetic: 11.7 us -> none  [body(): weighted.astype(jnp.bfloat16)]
    unnamed x19 -> x8, local copies, waits for them, and re-layouts: 9.48 us -> 0.02 us
    concatenate x4 -> x0, other arithmetic: 3.67 us -> none  [the longest x1 2.28 us: body(): jnp.concatenate(sent, axis=1)]
    transpose x1 -> x2, local copies, waits for them, and re-layouts: 0.02 us -> 2.87 us  [body(): numer.transpose(0, 2, 4, 1, 3).reshape(users, kv_part, GROUP, beam_part, HD)]
  transfers between devices with their start and end apart: 5 -> 0, of which waited for: 3 -> 0; matrix products, arithmetic and copies ran while one was open for 7% -> 0% of each run, Pallas kernels for 31% -> 0%
where the time goes in v1:
time: 123 us
  Pallas kernels  111 us (90%)
  local copies, waits for them, and re-layouts  6.87 us (6%)
  other arithmetic  2.82 us (2%)
  matrix products  1.62 us (1%)
    pallas_call x1, Pallas kernels, step(): pl.pallas_call(lambda *refs: step_kernel(plan, *refs), out_shape=[jax.Sha...  111 us
    transpose x2, local copies, waits for them, and re-layouts, body(): numer.transpose(0, 2, 4, 1, 3).reshape(users, kv_part, GROUP, beam_part, HD)  2.87 us

profile of v1, /device:TPU:0, one launch (start us, length us, event | category | flops | bytes accessed | tf_op | source)
XLA Modules:
  0.0 122.6 jit_solution(12167124595620693162)
XLA Ops:
  0.0 0.0 copy-start
  0.0 1.4 %subtract_clamp_fusion.refs_0_ = s32[8]{0:T(128)} fusion(s32[8]{0:T(128)} %param.12, s32[]{:T(128)S(6)} %mul.75), kind=kLoop, calls=%fused_computation.26 | loop fusion | flops 16 | bytes 68 | tf_op jit(solution)/shard_map/jit(clip)/min | solution.py:422
  1.4 1.7 %copy_bitcast_fusion.1 = bf16[8,16,8,128]{3,1,2,0:T(8,128)(2,1)} fusion(bf16[8,16,1024]{2,1,0:T(8,128)(2,1)} %param.7), kind=kLoop, calls=%fused_computation.11 | loop fusion | bytes 524288 | tf_op jit(solution)/shard_map/reshape | solution.py:424
  3.1 111.2 %step.1 = (f32[8,2,2,64,128]{4,3,2,1,0:T(8,128)}, f32[8,4,128]{2,1,0:T(4,128)}) custom-call(s32[8]{0:T(128)} %subtract_clamp_fusion.refs_0_, bf16[8,128,128]{2,1,0:T(8,128)(2,1)} %bitcast.39, bf16[8,512,1024]{2,1,0:T(8,128)(2,1)} %refs_2_.1, bf16[8,512,1024]{2,1,0:T(8,128)(2,1)} %refs_3_.1), custom_call_target="tpu_custom_call" | custom-call | flops 8589934592 | bytes 16777216 | tf_op jit(solution)/shard_map/step/pallas_call | solution.py:372
  114.2 1.6 %dynamic-slice_bitcast_fusion = f32[8,2,64,2,64]{2,4,1,3,0:T(8,128)S(1)} fusion(f32[8,2,2,64,128]{4,3,2,1,0:T(8,128)} %get-tuple-element.7, s32[]{:T(128)S(6)} %select_n.8), kind=kLoop, calls=%fused_computation | loop fusion | bytes 1048580 | tf_op jit(solution)/shard_map/transpose | solution.py:445
  115.8 0.0 copy-start.3
  115.8 0.0 copy-start.2
  115.8 1.3 %copy.29 = f32[8,2,64,2,64]{4,3,2,1,0:T(2,128)} copy(f32[8,2,64,2,64]{2,4,1,3,0:T(8,128)S(1)} %dynamic-slice_bitcast_fusion) | data formatting | bytes 1048576 | tf_op jit(solution)/shard_map/transpose | solution.py:445
  117.1 0.0 copy-start.1
  117.1 1.9 %reshape.77 = f32[8,8,16,128]{3,2,1,0:T(8,128)S(1)} reshape(f32[8,2,64,2,64]{4,3,2,1,0:T(2,128)} %copy.29) | data formatting | bytes 1048576 | tf_op jit(solution)/shard_map/reshape | solution.py:445
  119.0 0.0 copy-done.3
  119.0 0.1 constant_dynamic-slice_fusion
  119.1 0.1 reshape.78
  119.2 0.0 copy-done
  119.3 0.0 copy-done.2
  119.3 0.3 fusion.2
  119.6 0.1 reshape.79
  119.7 0.0 copy-done.1
  119.7 0.2 multiply_reduce_fusion
  120.0 1.3 %fusion = f32[8,16,256]{2,1,0:T(8,128)S(1)} fusion(bf16[1024,1024]{1,0:T(8,128)(2,1)} %param.11, s32[]{:T(128)S(6)} %select_n.9, s32[8,16]{1,0:T(8,128)S(1)} %copy-done.2), kind=kOutput, calls=%fused_computation.1 | convolution fusion | flops 67239936 | bytes 655876 | tf_op jit(solution)/shard_map/uwv,vc->uwc/dot_general | solution.py:428
  121.3 0.1 reshape.80
  121.5 1.2 copy_bitcast_fusion
  (9 shorter events, 0.1 us)
Async XLA Ops:
  0.0 119.3 %copy-start = (bf16[1024,1024]{1,0:T(8,128)(2,1)S(1)}, bf16[1024,1024]{1,0:T(8,128)(2,1)}, u32[]{:S(2)}) copy-start(bf16[1024,1024]{1,0:T(8,128)(2,1)} %param.10) | copy-start | bytes 6291460
  115.8 3.2 %copy-start.3 = (f32[8,4,128]{2,1,0:T(4,128)S(1)}, f32[8,4,128]{2,1,0:T(4,128)}, u32[]{:S(2)}) copy-start(f32[8,4,128]{2,1,0:T(4,128)} %get-tuple-element.8) | copy-start | bytes 49156
  115.8 3.4 %copy-start.2 = (s32[8,16]{1,0:T(8,128)S(1)}, s32[8,16]{1,0:T(8,128)}, u32[]{:S(2)}) copy-start(s32[8,16]{1,0:T(8,128)} %param.13) | copy-start | bytes 1540
  117.1 2.6 %copy-start.1 = (bf16[8,16,1024]{2,1,0:T(8,128)(2,1)S(1)}, bf16[8,16,1024]{2,1,0:T(8,128)(2,1)}, u32[]{:S(2)}) copy-start(bf16[8,16,1024]{2,1,0:T(8,128)(2,1)} %param.7) | copy-start | bytes 786436

commit v2 on v1

v2 whole, which is shorter than its diff:
```python
import math

import jax
import jax.numpy as jnp
import numpy as np
from jax import lax
from jax.experimental import pallas as pl
from jax.experimental.pallas import tpu as pltpu
from jax.sharding import PartitionSpec as P

HQ = 32
KH = 8
HD = 128
GROUP = HQ // KH
CORES = 2
LOG2E = math.log2(math.e)
FACTOR = HD ** (-0.5) * LOG2E
MESH = pl.DeviceIdType.MESH
STEPS = (
    ("diagonal", 2, 0, 3),
    ("finished", -17, 1, 0),
    ("delivered", -39, 4, 1),
    ("relay", 4, 1, 1),
    ("reduced", -17, 8, 0),
    ("paired", -3, 2, 0),
    ("columns", 7, 1, 4),
    ("crossed", -13, 8, 0),
    ("attend", 1, 0, 0),
)
NEEDS = (
    ("columns", "relay"), ("relay", "diagonal"), ("diagonal", "attend"), ("attend", "paired"), ("paired", "crossed"),
    ("crossed", "reduced"), ("reduced", "finished"), ("finished", "delivered"),
)


def upto(chunks, base, early, late, u, lib):
    some = base + u + lib.minimum(lib.maximum(u, 0), early) + late * lib.maximum(u - (chunks - 1), 0)
    return lib.minimum(lib.maximum(some, 0), chunks)


def turns(chunks):
    first = -max(base for _, base, _, _ in STEPS)
    last, order = first, {}
    while last < chunks or any(upto(chunks, *rest, last - 1, np) < chunks for _, *rest in STEPS):
        for name, *rest in STEPS:
            for v in range(upto(chunks, *rest, last - 1, np), upto(chunks, *rest, last, np)):
                order[name, v] = len(order)
        last += 1
    for before, after in NEEDS:
        assert all(order[before, v] < order[after, v] for v in range(chunks)), (before, after)
    return first, last


class Plan:
    def __init__(self, rows, cols):
        self.rows, self.cols = rows, cols
        self.planes = rows // CORES
        self.outer = 2 if self.planes % 2 == 0 else 1
        self.inner = self.planes // self.outer
        self.half = cols // 2
        names = []
        for s in range(1, cols):
            names += [("z", s), ("zr", s), ("zs", s)]
        for b in range(1, self.inner):
            names += [("bx", b), ("cd", b), ("x", b), ("xs", b)]
        for a in range(1, self.outer):
            names += [("by", a), ("ce", a), ("y", a), ("ys", a)]
            for b in range(1, self.inner):
                names += [(n, a, b) for n in ("ca", "cb", "dd", "ra", "ras", "rb", "rbs")]
        names += [("bd",), ("f",), ("fs",), ("fo",)]
        self.index = {name: at for at, name in enumerate(names)}


def step_kernel(
    plan, len_ref, tok_ref, q_hbm, k_hbm, v_hbm, kt_hbm, vt_hbm, out_ref,
    q_in, ktab, vtab, own_e, own_w, turned, turned_st, fin_st,
    q_all, part, from_pair, st, st_pair, sc, ra, ras, rb, rbs, xr, xrs, yr, yrs, zr, zrs, fin,
    kbuf, vbuf, send, recv, local,
):
    chunks = q_in.shape[0]
    outer, inner, cols, half = plan.outer, plan.inner, plan.cols, plan.half
    planes = plan.planes
    kv = KH // cols
    beams = q_in.shape[2]
    lines = GROUP * beams
    lanes = CORES * lines
    positions = k_hbm.shape[1]
    users = k_hbm.shape[0]
    vocab = ktab.shape[0]
    row, col = lax.axis_index("row"), lax.axis_index("col")
    k = lax.rem(row, CORES)
    pair = 1 - k
    me = row // CORES
    b_at, a_at = lax.rem(me, inner), me // inner
    offset = (row * cols + col) * positions

    def spot(a=0, b=0):
        return lax.rem(a_at + a + outer, outer) * inner + lax.rem(b_at + b + inner, inner)

    def at_spot(a=0, b=0):
        return {"row": spot(a, b) * CORES + k}

    def at_col(s):
        return {"col": lax.rem(col + s, cols)}

    at_pair = {"row": me * CORES + pair}
    in_x = range(1, inner)
    in_y = range(1, outer)
    in_xy = [(a, b) for a in in_y for b in in_x]
    in_z = range(1, cols)

    peers = [at_pair] + [at_col(s) for s in in_z] + [at_spot(0, b) for b in in_x] + [at_spot(a, 0) for a in in_y]

    def copy(v, name, src, dst, to):
        at = plan.index[name]
        return pltpu.make_async_remote_copy(
            src_ref=src, dst_ref=dst, send_sem=send.at[v, at], recv_sem=recv.at[v, at],
            device_id=to, device_id_type=MESH,
        )

    low, high = pl.ds(0, half), pl.ds(half, cols - half)

    def make(v, name):
        kind, *at = name
        if kind == "z":
            return copy(v, name, q_in.at[v], q_all.at[v, me, k, col], at_col(at[0]))
        if kind in ("bx", "by", "bd"):
            to = at_pair if kind == "bd" else at_spot(0, at[0]) if kind == "bx" else at_spot(at[0], 0)
            own = q_all.at[v, me, k]
            return copy(v, name, own, own, to)
        if kind == "cd":
            ref = q_all.at[v, spot(0, -at[0]), k]
            return copy(v, name, ref, ref, at_pair)
        if kind == "ce":
            ref = q_all.at[v, spot(-at[0], 0), k]
            return copy(v, name, ref, ref, at_pair)
        if kind == "ca":
            ref = q_all.at[v, spot(0, -at[1]), k, low]
            return copy(v, name, ref, ref, at_spot(at[0], 0))
        if kind == "cb":
            ref = q_all.at[v, spot(-at[0], 0), k, high]
            return copy(v, name, ref, ref, at_spot(0, at[1]))
        if kind == "dd":
            ref = q_all.at[v, spot(-at[0], -at[1]), k]
            return copy(v, name, ref, ref, at_pair)
        if kind == "f":
            return copy(v, name, part.at[v, pair], from_pair.at[v], at_pair)
        if kind == "fs":
            return copy(v, name, st.at[v], st_pair.at[v], at_pair)
        if kind == "ra":
            return copy(v, name, part.at[v, k, spot(*at), low], ra.at[v, at[0] - 1, at[1] - 1], at_spot(at[0], 0))
        if kind == "ras":
            return copy(v, name, sc.at[v, spot(*at), low], ras.at[v, at[0] - 1, at[1] - 1], at_spot(at[0], 0))
        if kind == "rb":
            return copy(v, name, part.at[v, k, spot(*at), high], rb.at[v, at[0] - 1, at[1] - 1], at_spot(0, at[1]))
        if kind == "rbs":
            return copy(v, name, sc.at[v, spot(*at), high], rbs.at[v, at[0] - 1, at[1] - 1], at_spot(0, at[1]))
        if kind == "x":
            return copy(v, name, part.at[v, k, spot(0, at[0])], xr.at[v, at[0] - 1], at_spot(0, at[0]))
        if kind == "xs":
            return copy(v, name, sc.at[v, spot(0, at[0])], xrs.at[v, at[0] - 1], at_spot(0, at[0]))
        if kind == "y":
            return copy(v, name, part.at[v, k, spot(at[0], 0)], yr.at[v, at[0] - 1], at_spot(at[0], 0))
        if kind == "ys":
            return copy(v, name, sc.at[v, spot(at[0], 0)], yrs.at[v, at[0] - 1], at_spot(at[0], 0))
        if kind == "zr":
            there = lax.rem(col + at[0], cols)
            return copy(v, name, part.at[v, k, me, there], zr.at[v, at[0] - 1], at_col(at[0]))
        if kind == "zs":
            there = lax.rem(col + at[0], cols)
            return copy(v, name, sc.at[v, me, there], zrs.at[v, at[0] - 1], at_col(at[0]))
        return copy(v, name, fin.at[v, k], fin.at[v, k], at_pair)

    def start(v, *names):
        for name in names:
            make(v, name).start()

    def arrived(v, *names):
        for name in names:
            make(v, name).wait_recv()

    def own_copy():
        return pltpu.make_async_copy(q_in, q_all.at[:, me, k, col], local.at[0])

    spare = 1 + 4 * cols
    wide = pl.ds(pl.multiple_of(col * kv * HD, HD), kv * HD)
    taken = [
        pltpu.make_async_copy(
            q_hbm.at[u, :, pl.ds((i * GROUP + g) * HD, HD)],
            q_in.at[u * kv + i, g],
            local.at[spare + (u * kv + i) * GROUP + g],
        )
        for u in range(users)
        for i in range(kv)
        for g in range(GROUP)
    ]
    spare += len(taken)
    tables = [
        pltpu.make_async_copy(kt_hbm.at[:, wide], ktab, local.at[spare]),
        pltpu.make_async_copy(vt_hbm.at[:, wide], vtab, local.at[spare + 1]),
    ]

    def own_terms(u, _):
        pick = lax.broadcasted_iota(jnp.int32, (vocab, beams), 0) == tok_ref[pl.ds(u, 1), :]
        pick = jnp.where(pick, 1.0, 0.0).astype(jnp.bfloat16)
        found, own_w[u] = (
            lax.dot_general(pick, tab[...], (((0,), (0,)), ((), ())), preferred_element_type=jnp.float32)
            for tab in (ktab, vtab)
        )
        for i in range(kv):
            keys = found[:, i * HD : (i + 1) * HD]
            for g in range(GROUP):
                q = q_in[u * kv + i, g].astype(jnp.float32)
                own_e[u * kv + i, g * beams : (g + 1) * beams] = jnp.sum(q * keys, axis=1, keepdims=True) * FACTOR
        return 0

    def fetch(v):
        slot = lax.rem(v, 2)
        found = []
        for c in range(cols):
            at = pl.ds(pl.multiple_of((c * kv + lax.rem(v, kv)) * HD, HD), HD)
            for n, (src, dst) in enumerate([(k_hbm, kbuf), (v_hbm, vbuf)]):
                found.append(
                    pltpu.make_async_copy(src.at[v // kv, :, at], dst.at[slot, c], local.at[1 + (c * 2 + n) * 2 + slot])
                )
        return found

    def start_fetch(v):
        for c in fetch(v):
            c.start()

    def columns(v):
        arrived(v, *[("z", s) for s in in_z])
        start(v, *[("bx", b) for b in in_x], *[("by", a) for a in in_y], ("bd",))

    def relay(v):
        for b in in_x:
            arrived(v, ("bx", b))
            start(v, *[("ca", a, b) for a in in_y], ("cd", b))
        for a in in_y:
            arrived(v, ("by", a))
            start(v, *[("cb", a, b) for b in in_x], ("ce", a))

    def diagonal(v):
        for a, b in in_xy:
            arrived(v, ("ca", a, b), ("cb", a, b))
            start(v, ("dd", a, b))

    def gathered(v):
        arrived(v, ("bd",), *[("cd", b) for b in in_x], *[("ce", a) for a in in_y])
        arrived(v, *[("dd", a, b) for a, b in in_xy])

    def heads(v, some):
        slot = lax.rem(v, 2)
        keep = lax.broadcasted_iota(jnp.int32, (positions, planes * lanes), 0) < len_ref[v // kv] - offset
        for c in some:
            q = q_all[v, :, :, c].reshape(planes * lanes, HD)
            s = lax.dot_general(kbuf[slot, c], q, (((1,), (1,)), ((), ())), preferred_element_type=jnp.float32)
            s = jnp.where(keep, s, -1e30)
            m = jnp.max(s, axis=0, keepdims=True)
            p = jnp.exp2((s - m) * FACTOR)
            total = jnp.sum(p, axis=0, keepdims=True)
            m = m * FACTOR
            o = lax.dot_general(
                vbuf[slot, c], p.astype(jnp.bfloat16), (((0,), (0,)), ((), ())), preferred_element_type=jnp.float32
            ).astype(jnp.bfloat16)
            for at in range(planes):
                span = slice(at * lanes, (at + 1) * lanes)
                st[v, at, c, :1, :] = m[:, span]
                st[v, at, c, 1:, :] = total[:, span]
                for h in range(2):
                    part[v, h, at, c] = o[h * (HD // 2) : (h + 1) * (HD // 2), span]

    def fuse(numers, stats):
        peaks = [x[..., :1, :] for x in stats]
        peak = peaks[0]
        for x in peaks[1:]:
            peak = jnp.maximum(peak, x)
        scales = [jnp.exp2(x - peak) for x in peaks]
        total = sum(x[..., 1:, :] * scale for x, scale in zip(stats, scales))
        numer = sum(x.astype(jnp.float32) * scale for x, scale in zip(numers, scales))
        return numer, peak, total

    def put(v, at, span, numer, peak, total):
        part[v, k, at, span] = numer.astype(jnp.bfloat16)
        sc[v, at, span, :1, :] = peak
        sc[v, at, span, 1:, :] = total

    def fuse_into(v, at, span, numers, stats):
        put(v, at, span, *fuse([part[v, k, at, span]] + numers, [sc[v, at, span]] + stats))

    def paired(v):
        arrived(v, ("f",), ("fs",))
        for at in range(planes):
            put(
                v, at, pl.ds(0, cols),
                *fuse([part[v, k, at], from_pair[v, at]], [st[v, at], st_pair[v, at]]),
            )
        for a, b in in_xy:
            start(v, ("ra", a, b), ("ras", a, b), ("rb", a, b), ("rbs", a, b))

    def crossed(v):
        for a, b in in_xy:
            arrived(v, ("ra", a, b), ("ras", a, b), ("rb", a, b), ("rbs", a, b))
        if in_xy:
            for b in in_x:
                fuse_into(
                    v, spot(0, b), low,
                    [ra[v, a - 1, b - 1] for a in in_y], [ras[v, a - 1, b - 1] for a in in_y],
                )
            for a in in_y:
                fuse_into(
                    v, spot(a, 0), high,
                    [rb[v, a - 1, b - 1] for b in in_x], [rbs[v, a - 1, b - 1] for b in in_x],
                )
        for b in in_x:
            start(v, ("x", b), ("xs", b))
        for a in in_y:
            start(v, ("y", a), ("ys", a))

    def reduced(v):
        for b in in_x:
            arrived(v, ("x", b), ("xs", b))
        for a in in_y:
            arrived(v, ("y", a), ("ys", a))
        fuse_into(
            v, me, pl.ds(0, cols),
            [xr[v, b - 1] for b in in_x] + [yr[v, a - 1] for a in in_y],
            [xrs[v, b - 1] for b in in_x] + [yrs[v, a - 1] for a in in_y],
        )
        for s in in_z:
            start(v, ("zr", s), ("zs", s))

    def finished(v):
        for s in in_z:
            arrived(v, ("zr", s), ("zs", s))
        numer, peak, total = fuse(
            [part[v, k, me, col]] + [zr[v, s - 1] for s in in_z],
            [sc[v, me, col]] + [zrs[v, s - 1] for s in in_z],
        )
        fin[v, k] = numer
        fin_st[v, :1] = peak
        fin_st[v, 1:2] = total
        start(v, ("fo",))

    def delivered(v):
        arrived(v, ("fo",))
        turned[...] = fin[v].reshape(HD, lanes).T
        turned_st[...] = fin_st[v].T
        mine = pl.ds(pl.multiple_of(k * lines, lines), lines)
        numer = turned[mine, :]
        peak, total = turned_st[mine, 0:1], turned_st[mine, 1:2]
        own = own_e[v]
        top = jnp.maximum(peak, own)
        carried, fresh = jnp.exp2(peak - top), jnp.exp2(own - top)
        u, i = v // kv, lax.rem(v, kv)
        value = own_w[u, :, pl.ds(pl.multiple_of(i * HD, HD), HD)]
        bottom = total * carried + fresh
        for g in range(GROUP):
            span = slice(g * beams, (g + 1) * beams)
            done = (numer[span] * carried[span] + fresh[span] * value) / bottom[span]
            head = pl.ds(pl.multiple_of((i * GROUP + g) * HD, HD), HD)
            out_ref[u, :, head] = done.astype(jnp.bfloat16)

    for c in taken + tables:
        c.start()
    start_fetch(0)
    barrier = pltpu.get_barrier_semaphore()
    for to in peers:
        pl.semaphore_signal(barrier, inc=1, device_id=to, device_id_type=MESH)
    pl.semaphore_wait(barrier, len(peers))

    def send_queries(v, _):
        start(v, *[("z", s) for s in in_z])
        return 0

    for c in taken:
        c.wait()
    own_copy().start()
    lax.fori_loop(0, chunks, send_queries, 0)
    for c in tables:
        c.wait()
    lax.fori_loop(0, users, own_terms, 0)
    own_copy().wait()

    def attend(v):
        @pl.when(v + 1 < chunks)
        def _():
            start_fetch(v + 1)

        gathered(v)
        for c in fetch(v):
            c.wait()
        heads(v, range(cols))
        start(v, ("f",), ("fs",))

    run = dict(
        columns=columns, relay=relay, diagonal=diagonal, attend=attend, paired=paired, crossed=crossed,
        reduced=reduced, finished=finished, delivered=delivered,
    )

    def turn(u, _):
        for name, base, early, late in STEPS:
            def one(v, _, name=name):
                run[name](v)
                return 0

            ends = [upto(chunks, base, early, late, x, jnp) for x in (u - 1, u)]
            lax.fori_loop(*ends, one, 0)
        return 0

    lax.fori_loop(*turns(chunks), turn, 0)

    def close(v, _):
        for name in plan.index:
            make(v, name).wait_send()
        return 0

    lax.fori_loop(0, chunks, close, 0)


def body(queries, key_cache, value_cache, key_table, value_table, lengths, token_ids):
    rows, cols = lax.axis_size("row"), lax.axis_size("col")
    plan = Plan(rows, cols)
    users, beams, _ = queries.shape
    positions = key_cache.shape[1]
    vocab = key_table.shape[0]
    kv = KH // cols
    chunks = users * kv
    lines = GROUP * beams
    lanes = CORES * lines
    outer, inner, planes, half = plan.outer, plan.inner, plan.planes, plan.half
    deep = HD // 2
    f32, bf16 = jnp.float32, jnp.bfloat16
    vmem = pl.BlockSpec(memory_space=pltpu.VMEM)
    hbm = pl.BlockSpec(memory_space=pl.ANY)
    block, stat = (deep, lanes), (2, lanes)

    def numer(*lead):
        return pltpu.VMEM((chunks, *lead, *block), bf16)

    def stats(*lead):
        return pltpu.VMEM((chunks, *lead, *stat), f32)

    x, y = max(inner - 1, 1), max(outer - 1, 1)
    copies = len(plan.index)
    scores = chunks * cols * planes * lanes * positions
    return pl.pallas_call(
        lambda *refs: step_kernel(plan, *refs),
        out_shape=jax.ShapeDtypeStruct(queries.shape, bf16),
        in_specs=[pl.BlockSpec(memory_space=pltpu.SMEM), vmem, hbm, hbm, hbm, hbm, hbm],
        out_specs=vmem,
        scratch_shapes=[
            pltpu.VMEM((chunks, GROUP, beams, HD), bf16),
            pltpu.VMEM((vocab, kv * HD), bf16),
            pltpu.VMEM((vocab, kv * HD), bf16),
            pltpu.VMEM((chunks, lines, 1), f32),
            pltpu.VMEM((users, beams, kv * HD), f32),
            pltpu.VMEM((lanes, HD), f32),
            pltpu.VMEM((lanes, 8), f32),
            pltpu.VMEM((chunks, 8, lanes), f32),
            pltpu.VMEM((chunks, planes, CORES, cols, GROUP, beams, HD), bf16),
            numer(2, planes, cols),
            numer(planes, cols),
            stats(planes, cols),
            stats(planes, cols),
            stats(planes, cols),
            numer(y, x, half),
            stats(y, x, half),
            numer(y, x, cols - half),
            stats(y, x, cols - half),
            numer(x, cols),
            stats(x, cols),
            numer(y, cols),
            stats(y, cols),
            numer(cols - 1),
            stats(cols - 1),
            pltpu.VMEM((chunks, 2, *block), f32),
            pltpu.VMEM((2, cols, positions, HD), bf16),
            pltpu.VMEM((2, cols, positions, HD), bf16),
            pltpu.SemaphoreType.DMA((chunks, copies)),
            pltpu.SemaphoreType.DMA((chunks, copies)),
            pltpu.SemaphoreType.DMA((1 + 4 * cols + chunks * GROUP + 2,)),
        ],
        compiler_params=pltpu.CompilerParams(
            collective_id=0, has_side_effects=True, vmem_limit_bytes=60 * 1024 * 1024
        ),
        cost_estimate=pl.CostEstimate(
            flops=4 * scores * HD, bytes_accessed=4 * key_cache.size, transcendentals=scores
        ),
        name="step",
    )(lengths, token_ids, queries, key_cache, value_cache, key_table, value_table)


def solution(mesh):
    return jax.shard_map(
        body,
        mesh=mesh,
        in_specs=(
            P(None, "row", "col"),
            P(None, ("row", "col"), None),
            P(None, ("row", "col"), None),
            P(),
            P(),
            P(),
            P(None, "row"),
        ),
        out_specs=P(None, "row", "col"),
        check_vma=False,
    )
```

time: 123 us -> 100 us (0.81)
  Pallas kernels: 111 us -> 98.6 us
  local copies, waits for them, and re-layouts: 6.87 us -> 1.67 us
  other arithmetic: 2.82 us -> 0 us
  matrix products: 1.62 us -> 0 us
    pallas_call x1, Pallas kernels: 111 us -> 98.6 us  [body(): pl.pallas_call(lambda *refs: step_kernel(plan, *refs), out_shape=jax.Shap...]
    reshape x5 -> x0, local copies, waits for them, and re-layouts: 3.79 us -> none  [the longest x1 1.86 us: body(): numer.transpose(0, 2, 4, 1, 3).reshape(users, kv_part, GROUP, beam_part, HD)]
    transpose x4 -> x0, local copies, waits for them, and re-layouts: 2.89 us -> none  [the longest x2 2.87 us: body(): numer.transpose(0, 2, 4, 1, 3).reshape(users, kv_part, GROUP, beam_part, HD)]
    unnamed x8 -> x1, local copies, waits for them, and re-layouts: 0.02 us -> 1.67 us
    dot_general x2 -> x0, matrix products: 1.62 us -> none  [body(): jnp.einsum('uwv,vc->uwc', (token_ids[..., None] == jnp.arange(table.shape...]
    min x1 -> x0, other arithmetic: 1.38 us -> none  [body(): live = jnp.clip(lengths - offset, 0, positions)]
where the time goes in v2:
time: 100 us
  Pallas kernels  98.6 us (99%)
  local copies, waits for them, and re-layouts  1.67 us (2%)
    pallas_call x1, Pallas kernels, body(): pl.pallas_call(lambda *refs: step_kernel(plan, *refs), out_shape=jax.Shap...  98.6 us

profile of v2, /device:TPU:0, one launch (start us, length us, event | category | flops | bytes accessed | tf_op | source)
XLA Modules:
  0.0 100.3 jit_solution(12183489393801990054)
XLA Ops:
  0.0 98.6 %step.1 = bf16[8,16,1024]{2,1,0:T(8,128)(2,1)} custom-call(s32[8]{0:T(128)} %refs_0_.1, s32[8,16]{1,0:T(8,128)} %refs_1_.1, bf16[8,16,1024]{2,1,0:T(8,128)(2,1)} %refs_2_.1, bf16[8,512,1024]{2,1,0:T(8,128)(2,1)} %refs_3_.1, bf16[8,512,1024]{2,1,0:T(8,128)(2,1)} %refs_4_.1, bf16[1024,1024]{1,0:T(8,128)(2,1)} %refs_5_.1, bf16[1024,1024]{1,0:T(8,128)(2,1)} %refs_6_.1), custom_call_target="tpu_custom_call" | custom-call | flops 8589934592 | bytes 16777216 | tf_op jit(solution)/shard_map/step/pallas_call | solution.py:448
  98.6 1.7 %copy.9 = bf16[8,16,1024]{2,1,0:T(8,128)(2,1)} copy(bf16[8,16,1024]{2,1,0:T(8,128)(2,1)} %step.1) | data formatting | bytes 524288

commit v3 on v2

--- a/solution.py
+++ b/solution.py
@@ -16,16 +16,19 @@
 LOG2E = math.log2(math.e)
 FACTOR = HD ** (-0.5) * LOG2E
 MESH = pl.DeviceIdType.MESH
+PLANE_FIRST = 3
+PLANE_CROSS = 2
+PLANE_COLUMNS = 4
 STEPS = (
-    ("diagonal", 2, 0, 3),
-    ("finished", -17, 1, 0),
-    ("delivered", -39, 4, 1),
-    ("relay", 4, 1, 1),
-    ("reduced", -17, 8, 0),
-    ("paired", -3, 2, 0),
-    ("columns", 7, 1, 4),
-    ("crossed", -13, 8, 0),
+    ("paired", -1, 0, 1),
+    ("relay", 4, 0, 2),
+    ("columns", 7, 2, 2),
+    ("crossed", -7, 4, 1),
+    ("diagonal", 2, 0, 4),
     ("attend", 1, 0, 0),
+    ("reduced", -8, 2, 2),
+    ("delivered", -16, 2, 1),
+    ("finished", -14, 4, 1),
 )
 NEEDS = (
     ("columns", "relay"), ("relay", "diagonal"), ("diagonal", "attend"), ("attend", "paired"), ("paired", "crossed"),
@@ -69,6 +72,11 @@
                 names += [(n, a, b) for n in ("ca", "cb", "dd", "ra", "ras", "rb", "rbs")]
         names += [("bd",), ("f",), ("fs",), ("fo",)]
         self.index = {name: at for at, name in enumerate(names)}
+        self.same = [n for n in names if n[0] not in ("z", "bx", "by", "bd", "ca", "cb", "cd", "ce", "dd")]
+        self.usual = [n for n in names if n not in self.same]
+        other = {"z": "pz", "bx": "px", "by": "py", "bd": "pd", "ca": "pca", "cb": "pcb"}
+        self.plane = [(other[n[0]], *n[1:]) for n in self.usual if n[0] in other]
+        self.index |= {(other[n[0]], *n[1:]): self.index[n] for n in self.usual if n[0] in other}
 
 
 def step_kernel(
@@ -119,6 +127,8 @@
         )
 
     low, high = pl.ds(0, half), pl.ds(half, cols - half)
+    first_groups, last_groups = pl.ds(0, GROUP // 2), pl.ds(GROUP // 2, GROUP - GROUP // 2)
+    turned_at = chunks - min(PLANE_FIRST, chunks // 4)
 
     def make(v, name):
         kind, *at = name
@@ -128,6 +138,21 @@
             to = at_pair if kind == "bd" else at_spot(0, at[0]) if kind == "bx" else at_spot(at[0], 0)
             own = q_all.at[v, me, k]
             return copy(v, name, own, own, to)
+        if kind in ("px", "py"):
+            own = q_all.at[v, me, k, col]
+            return copy(v, name, own, own, at_spot(0, at[0]) if kind == "px" else at_spot(at[0], 0))
+        if kind == "pca":
+            ref = q_all.at[v, spot(0, -at[1]), k, col, first_groups]
+            return copy(v, name, ref, ref, at_spot(at[0], 0))
+        if kind == "pcb":
+            ref = q_all.at[v, spot(-at[0], 0), k, col, last_groups]
+            return copy(v, name, ref, ref, at_spot(0, at[1]))
+        if kind == "pz":
+            ref = q_all.at[v, :, k, col]
+            return copy(v, name, ref, ref, at_col(at[0]))
+        if kind == "pd":
+            ref = q_all.at[v, :, k]
+            return copy(v, name, ref, ref, at_pair)
         if kind == "cd":
             ref = q_all.at[v, spot(0, -at[0]), k]
             return copy(v, name, ref, ref, at_pair)
@@ -229,26 +254,57 @@
         for c in fetch(v):
             c.start()
 
+    def either(v, usual, plane):
+        pl.when(v < turned_at)(usual)
+        pl.when(v >= turned_at)(plane)
+
+    def plane_cross(v):
+        for b in in_x:
+            arrived(v, ("px", b))
+            start(v, *[("pca", a, b) for a in in_y])
+        for a in in_y:
+            arrived(v, ("py", a))
+            start(v, *[("pcb", a, b) for b in in_x])
+
+    def plane_columns(v):
+        for a, b in in_xy:
+            arrived(v, ("pca", a, b), ("pcb", a, b))
+        start(v, *[("pz", s) for s in in_z])
+
     def columns(v):
-        arrived(v, *[("z", s) for s in in_z])
-        start(v, *[("bx", b) for b in in_x], *[("by", a) for a in in_y], ("bd",))
+        @pl.when(v < turned_at)
+        def _():
+            arrived(v, *[("z", s) for s in in_z])
+            start(v, *[("bx", b) for b in in_x], *[("by", a) for a in in_y], ("bd",))
 
     def relay(v):
-        for b in in_x:
-            arrived(v, ("bx", b))
-            start(v, *[("ca", a, b) for a in in_y], ("cd", b))
-        for a in in_y:
-            arrived(v, ("by", a))
-            start(v, *[("cb", a, b) for b in in_x], ("ce", a))
+        @pl.when(v < turned_at)
+        def _():
+            for b in in_x:
+                arrived(v, ("bx", b))
+                start(v, *[("ca", a, b) for a in in_y], ("cd", b))
+            for a in in_y:
+                arrived(v, ("by", a))
+                start(v, *[("cb", a, b) for b in in_x], ("ce", a))
 
     def diagonal(v):
-        for a, b in in_xy:
-            arrived(v, ("ca", a, b), ("cb", a, b))
-            start(v, ("dd", a, b))
+        def usual():
+            for a, b in in_xy:
+                arrived(v, ("ca", a, b), ("cb", a, b))
+                start(v, ("dd", a, b))
+
+        def plane():
+            arrived(v, *[("pz", s) for s in in_z])
+            start(v, ("pd",))
+
+        either(v, usual, plane)
 
     def gathered(v):
-        arrived(v, ("bd",), *[("cd", b) for b in in_x], *[("ce", a) for a in in_y])
-        arrived(v, *[("dd", a, b) for a, b in in_xy])
+        def usual():
+            arrived(v, ("bd",), *[("cd", b) for b in in_x], *[("ce", a) for a in in_y])
+            arrived(v, *[("dd", a, b) for a, b in in_xy])
+
+        either(v, usual, lambda: arrived(v, ("pd",)))
 
     def heads(v, some):
         slot = lax.rem(v, 2)
@@ -377,11 +433,17 @@
     for c in taken:
         c.wait()
     own_copy().start()
-    lax.fori_loop(0, chunks, send_queries, 0)
+    lax.fori_loop(0, turned_at, send_queries, 0)
+    own_copy().wait()
+
+    def send_plane(v, _):
+        start(v, *[("px", b) for b in in_x], *[("py", a) for a in in_y])
+        return 0
+
+    lax.fori_loop(turned_at, chunks, send_plane, 0)
     for c in tables:
         c.wait()
     lax.fori_loop(0, users, own_terms, 0)
-    own_copy().wait()
 
     def attend(v):
         @pl.when(v + 1 < chunks)
@@ -399,7 +461,18 @@
         reduced=reduced, finished=finished, delivered=delivered,
     )
 
+    begin, end = turns(chunks)
+
+    def each(step):
+        def one(v, _):
+            step(v)
+            return 0
+
+        lax.fori_loop(turned_at, chunks, one, 0)
+
     def turn(u, _):
+        pl.when(u == begin + PLANE_CROSS)(lambda: each(plane_cross))
+        pl.when(u == begin + PLANE_COLUMNS)(lambda: each(plane_columns))
         for name, base, early, late in STEPS:
             def one(v, _, name=name):
                 run[name](v)
@@ -409,11 +482,15 @@
             lax.fori_loop(*ends, one, 0)
         return 0
 
-    lax.fori_loop(*turns(chunks), turn, 0)
+    lax.fori_loop(begin, end, turn, 0)
 
     def close(v, _):
-        for name in plan.index:
-            make(v, name).wait_send()
+        def sent(names):
+            for name in names:
+                make(v, name).wait_send()
+
+        sent(plan.same)
+        either(v, lambda: sent(plan.usual), lambda: sent(plan.plane))
         return 0
 
     lax.fori_loop(0, chunks, close, 0)
@@ -443,7 +520,7 @@
         return pltpu.VMEM((chunks, *lead, *stat), f32)
 
     x, y = max(inner - 1, 1), max(outer - 1, 1)
-    copies = len(plan.index)
+    copies = len(plan.same + plan.usual)
     scores = chunks * cols * planes * lanes * positions
     return pl.pallas_call(
         lambda *refs: step_kernel(plan, *refs),

time: 100 us -> 98.5 us (0.985)
  Pallas kernels: 98.6 us -> 96.7 us
    pallas_call x1, Pallas kernels: 98.6 us -> 96.7 us  [body(): pl.pallas_call(lambda *refs: step_kernel(plan, *refs), out_shape=jax.Shap...]
where the time goes in v3:
time: 98.5 us; the launch traced here: 98.4 us
  Pallas kernels  96.7 us (98%)
  local copies, waits for them, and re-layouts  1.67 us (2%)
    pallas_call x1, Pallas kernels, body(): pl.pallas_call(lambda *refs: step_kernel(plan, *refs), out_shape=jax.Shap...  96.7 us

profile of v3, /device:TPU:0, one launch (start us, length us, event | category | flops | bytes accessed | tf_op | source)
XLA Modules:
  0.0 98.4 jit_solution(8395089613313906735)
XLA Ops:
  0.0 96.7 %step.1 = bf16[8,16,1024]{2,1,0:T(8,128)(2,1)} custom-call(s32[8]{0:T(128)} %refs_0_.1, s32[8,16]{1,0:T(8,128)} %refs_1_.1, bf16[8,16,1024]{2,1,0:T(8,128)(2,1)} %refs_2_.1, bf16[8,512,1024]{2,1,0:T(8,128)(2,1)} %refs_3_.1, bf16[8,512,1024]{2,1,0:T(8,128)(2,1)} %refs_4_.1, bf16[1024,1024]{1,0:T(8,128)(2,1)} %refs_5_.1, bf16[1024,1024]{1,0:T(8,128)(2,1)} %refs_6_.1), custom_call_target="tpu_custom_call" | custom-call | flops 8589934592 | bytes 16777216 | tf_op jit(solution)/shard_map/step/pallas_call | solution.py:525
  96.7 1.7 %copy.9 = bf16[8,16,1024]{2,1,0:T(8,128)(2,1)} copy(bf16[8,16,1024]{2,1,0:T(8,128)(2,1)} %step.1) | data formatting | bytes 524288

commit v4 on v3

--- a/solution.py
+++ b/solution.py
@@ -16,7 +16,7 @@
 LOG2E = math.log2(math.e)
 FACTOR = HD ** (-0.5) * LOG2E
 MESH = pl.DeviceIdType.MESH
-PLANE_FIRST = 3
+PLANE_FIRST = 4
 PLANE_CROSS = 2
 PLANE_COLUMNS = 4
 STEPS = (

time: 98.5 us -> 98.3 us (level)
  no operation moved by 1% of the time
where the time goes in v4:
time: 98.3 us; the launch traced here: 98.1 us
  Pallas kernels  96.4 us (98%)
  local copies, waits for them, and re-layouts  1.67 us (2%)
    pallas_call x1, Pallas kernels, body(): pl.pallas_call(lambda *refs: step_kernel(plan, *refs), out_shape=jax.Shap...  96.4 us

profile of v4, /device:TPU:0, one launch (start us, length us, event | category | flops | bytes accessed | tf_op | source)
XLA Modules:
  0.0 98.1 jit_solution(411037677779212179)
XLA Ops:
  0.0 96.4 %step.1 = bf16[8,16,1024]{2,1,0:T(8,128)(2,1)} custom-call(s32[8]{0:T(128)} %refs_0_.1, s32[8,16]{1,0:T(8,128)} %refs_1_.1, bf16[8,16,1024]{2,1,0:T(8,128)(2,1)} %refs_2_.1, bf16[8,512,1024]{2,1,0:T(8,128)(2,1)} %refs_3_.1, bf16[8,512,1024]{2,1,0:T(8,128)(2,1)} %refs_4_.1, bf16[1024,1024]{1,0:T(8,128)(2,1)} %refs_5_.1, bf16[1024,1024]{1,0:T(8,128)(2,1)} %refs_6_.1), custom_call_target="tpu_custom_call" | custom-call | flops 8589934592 | bytes 16777216 | tf_op jit(solution)/shard_map/step/pallas_call | solution.py:525
  96.5 1.7 %copy.9 = bf16[8,16,1024]{2,1,0:T(8,128)(2,1)} copy(bf16[8,16,1024]{2,1,0:T(8,128)(2,1)} %step.1) | data formatting | bytes 524288
